TPU v7x, 128 devices: a whole 4x4x4 slice. The times are simulated.
128 devices in a mesh: gx: 8 (over z_hi, y), gz: 16 (over z_lo, x, core).
Axes of the slice: x: 4, y: 4, z: 4 (z_hi: 2, z_lo: 2; z = z_hi * 2 + z_lo), core: 2. Of those that a mesh axis runs over, the one named last changes fastest.
Arguments:
- high_u: bfloat16 [256, 512, 512], P('gx', 'gz'), may hold values from -6 to 6
- high_v: bfloat16 [256, 512, 512], P('gx', 'gz'), may hold values from -6 to 6
- low_u: bfloat16 [2048, 512], P(('gx', 'gz')), may hold values from -0.25 to 0.25
- low_v: bfloat16 [2048, 512], P(('gx', 'gz')), may hold values from -0.25 to 0.25
- low_kx: int32 [2048], P(('gx', 'gz')), may hold values from 0 to 64, as said below
- low_kz: int32 [2048], P(('gx', 'gz')), may hold values from 0 to 64, as said below
- tau_inverse: bfloat16 [2048, 512, 512], P(('gx', 'gz')), may hold values from -0.25 to 0.25
Outputs:
- high_term: bfloat16 [256, 512, 512], P('gx', 'gz')
- low_response: float32 [2048, 512], P(('gx', 'gz'))
Inputs may be any that keep to these rules, and one draw needn't show every extreme that they name: Slot m holds the retained mode (low_kx[m], low_kz[m]); no two slots hold the same pair; the device that holds slot m owns that mode. `low_kz`: paired with low_kx slot by slot.
All inputs are finite; a program needn't handle non-finite values.
Results may differ from a plain program's by a relative error of at most 0.0047.
Values may be sent and summed in bfloat16 or wider, within the bound.
No kernel may reach another device: no remote copies, remote signals or barrier semaphores. Data moves between devices by JAX's collectives and lax.ppermute only.
A program may use at most 128 MiB of HBM per device.

v0:
```python
import math
import jax
import jax.numpy as jnp
from jax import lax
from jax.sharding import PartitionSpec as P

KL = 32
CONTRACT_FIRST = (((0,), (0,)), ((), ()))


def in_one_piece(arrays, axis, dim, along):
    columns = [a.reshape(*a.shape[:along], -1) for a in arrays]
    both = jnp.concatenate(columns, axis=along)
    whole, at, done = (lax.all_gather(both, axis, axis=dim, tiled=True), 0, [])
    for a, column in zip(arrays, columns):
        section = whole[..., at : at + column.shape[along]]
        done.append(section.reshape(*section.shape[:along], *a.shape[along:]))
        at += column.shape[along]
    return tuple(done)


def cut_along(x, dim, count):
    shape = x.shape
    pieces = x.reshape(*shape[:dim], count, shape[dim] // count, *shape[dim + 1 :])
    return jnp.moveaxis(pieces, dim, 0)


def sent_and_summed(x, axis, dim):
    count = lax.axis_size(axis)
    pieces = lax.all_to_all(cut_along(x, dim, count), axis, 0, 0, tiled=True)
    return jnp.sum(pieces, axis=0)


def axis_table(index, positions, length):
    wavenum = jnp.where(index <= KL, index, index - KL)
    phases = wavenum[:, None] * positions[None, :] % length
    angles = phases.astype(jnp.float32) * (2.0 * math.pi / length)
    return jnp.where((index <= KL)[:, None], jnp.cos(angles), jnp.sin(angles))


def mode_weight(index_x, index_z):
    return jnp.where(index_x > 0, 2.0, 1.0).astype(jnp.float32) * jnp.where(
        index_z > 0, 2.0, 1.0
    ).astype(jnp.float32)


def on_device(high_u, high_v, low_u, low_v, low_kx, low_kz, tau_inverse):
    cells_x, cells_z, levels = high_u.shape
    owned_modes = low_u.shape[0]
    groups_x = lax.axis_size("gx")
    groups_z = lax.axis_size("gz")
    length_x = groups_x * cells_x
    length_z = groups_z * cells_z
    points = cells_x * cells_z
    unitary = 1.0 / math.sqrt(length_x * length_z)
    where_x = lax.axis_index("gx") * cells_x + jnp.arange(cells_x, dtype=jnp.int32)
    where_z = lax.axis_index("gz") * cells_z + jnp.arange(cells_z, dtype=jnp.int32)

    def patterns(index_x, index_z):
        table_x = axis_table(index_x, where_x, length_x)
        table_z = axis_table(index_z, where_z, length_z)
        return (
            (table_x[:, :, None] * table_z[:, None, :])
            .reshape(index_x.shape[0], points)
            .astype(jnp.bfloat16)
        )

    shard_u, shard_v, shard_x, shard_z = in_one_piece(
        (low_u, low_v, low_kx.astype(jnp.bfloat16), low_kz.astype(jnp.bfloat16)), ("gx", "gz"), 0, 1
    )
    index_x = shard_x.astype(jnp.int32)
    index_z = shard_z.astype(jnp.int32)
    stacked = jnp.concatenate([shard_u, shard_v], axis=1)
    coarse = lax.dot_general(
        patterns(index_x, index_z), stacked, CONTRACT_FIRST, preferred_element_type=jnp.float32
    )
    add_every_x = index_x
    add_every_z = index_z
    coarse, every_x, every_z = (coarse, add_every_x, add_every_z)
    fine_u = high_u.reshape(points, levels)
    fine_v = high_v.reshape(points, levels)
    coarse_u = coarse[:, :levels]
    coarse_v = coarse[:, levels:]
    self_term = (coarse_u * coarse_v + fine_u.astype(jnp.float32) * fine_v).astype(jnp.bfloat16)
    cross_term = coarse_u * fine_v + fine_u * coarse_v
    cross_round = cross_term.astype(jnp.bfloat16)
    own_weight = mode_weight(low_kx, low_kz)[:, None]
    products = jnp.concatenate([self_term, cross_round], axis=1)
    serial = jnp.arange(owned_modes * groups_x * lax.axis_size("gz"), dtype=jnp.int32)
    column = serial // (owned_modes * groups_x)
    row_group = serial // owned_modes % groups_x
    modes = (row_group * groups_z + column) * owned_modes + serial % owned_modes
    table = patterns(jnp.take(every_x, modes), jnp.take(every_z, modes))
    column_part = lax.psum_scatter(
        jnp.dot(table, products, preferred_element_type=jnp.float32) * unitary,
        "gz",
        scatter_dimension=0,
        tiled=True,
    )
    totals = sent_and_summed(column_part, "gx", 0)
    forcing = totals[:, :levels]
    cross_low = (own_weight * totals[:, levels:]).astype(jnp.bfloat16)
    index_x = every_x
    index_z = every_z
    restored = lax.dot_general(
        patterns(index_x, index_z),
        lax.all_gather(cross_low, ("gx", "gz"), axis=0, tiled=True),
        CONTRACT_FIRST,
        preferred_element_type=jnp.float32,
    )
    high_term = (
        (cross_term - unitary * restored).astype(jnp.bfloat16).reshape(cells_x, cells_z, levels)
    )
    low_response = jnp.einsum(
        "mij,mj->mi", tau_inverse, forcing.astype(jnp.bfloat16), preferred_element_type=jnp.float32
    )
    return (high_term, low_response)


def solution(mesh):
    placed = (
        P("gx", "gz", None),
        P("gx", "gz", None),
        P(("gx", "gz"), None),
        P(("gx", "gz"), None),
        P(("gx", "gz")),
        P(("gx", "gz")),
        P(("gx", "gz"), None, None),
    )
    return jax.shard_map(
        on_device,
        mesh=mesh,
        in_specs=placed,
        out_specs=(P("gx", "gz", None), P(("gx", "gz"), None)),
        check_vma=False,
    )
```

profile of v0, /device:TPU:1, one launch (start us, length us, event | category | flops | bytes accessed | tf_op | source)
XLA Modules:
  0.0 554.5 jit_solution(8208175064779380195)
XLA Ops:
  7.2 0.0 all-gather.3.cloned.1.call-start
  7.2 0.7 convert_bitcast_fusion.1
  7.9 0.1 copy.11
  8.0 0.7 convert_bitcast_fusion
  8.6 0.1 copy.12
  8.7 1.4 concatenate.9
  10.2 0.0 all-gather.3.cloned.1.call-update
  10.2 0.0 reduce-scatter.2.cloned.1.call-start
  10.3 201.3 %all-gather.3.cloned.1.call-done = bf16[2048,1026]{1,0:T(8,128)(2,1)} async-done(((bf16[16,1026]{1,0:T(8,128)(2,1)}), bf16[2048,1026]{1,0:T(8,128)(2,1)}) %all-gather.3.cloned.1.call-update) | async-done | bytes 4202512 | tf_op jit(solution)/shard_map/all_gather | solution.py:14
  211.6 2.5 convert_reduce_fusion.1
  214.1 11.8 %gather_fusion.1 = s32[2048]{0:T(1024)S(1)} fusion(s32[2048]{0:T(1024)S(1)} %get-tuple-element.5, s32[2048]{0:T(1024)S(1)} %broadcast_clamp_fusion), kind=kCustom, calls=%fused_computation.1.clone | custom fusion | bytes 24576 | tf_op jit(solution)/shard_map/jit(_take)/gather | solution.py:93
  226.0 11.8 %gather_fusion = s32[2048]{0:T(1024)S(1)} fusion(s32[2048]{0:T(1024)S(1)} %get-tuple-element.3, s32[2048]{0:T(1024)S(1)} %broadcast_clamp_fusion), kind=kCustom, calls=%fused_computation.clone | custom fusion | bytes 24576 | tf_op jit(solution)/shard_map/jit(_take)/gather | solution.py:93
  237.8 2.0 fusion.8
  239.8 4.2 sine_select_fusion
  244.0 1.1 multiply_convert_fusion.1
  245.1 1.1 multiply_convert_fusion
  246.2 0.9 copy-done
  247.1 0.0 copy-start.2
  247.1 4.5 fusion
  251.6 1.1 fusion.44
  252.7 7.2 %convolution_multiply_fusion = f32[2048,1024]{1,0:T(8,128)} fusion(bf16[2048,1024]{0,1:T(8,128)(2,1)S(1)} %bitcast.30, bf16[1024,512]{1,0:T(8,128)(2,1)S(1)} %get-tuple-element.9, bf16[1024,512]{1,0:T(8,128)(2,1)S(1)} %get-tuple-element.11), kind=kOutput, calls=%fused_computation.4 | convolution fusion | flops 4301258752 | bytes 14680064 | tf_op jit(solution)/shard_map/dot_general | solution.py:95
  259.9 0.0 reduce-scatter.2.cloned.1.call-update
  260.0 69.8 %reduce-scatter.2.cloned.1.call-done = f32[128,1024]{1,0:T(8,128)} async-done(((f32[2048,1024]{1,0:T(8,128)}), f32[128,1024]{1,0:T(8,128)}) %reduce-scatter.2.cloned.1.call-update) | async-done | bytes 524304 | tf_op jit(solution)/shard_map/reduce_scatter | solution.py:94
  329.8 6.6 %all-to-all-start = ((f32[8,16,1024]{2,1,0:T(8,128)}), f32[8,16,1024]{2,1,0:T(8,128)S(1)}, u32[]{:S(2)}, u32[]{:S(2)}) async-start(f32[8,16,1024]{2,1,0:T(8,128)} %bitcast.33), calls=%async_computation.1 | async-start | bytes 1048576 | tf_op jit(solution)/shard_map/all_to_all | solution.py:30
  336.4 0.0 all-gather.5.cloned.1.call-start
  336.5 9.0 %all-to-all-done = f32[8,16,1024]{2,1,0:T(8,128)S(1)} async-done(((f32[8,16,1024]{2,1,0:T(8,128)}), f32[8,16,1024]{2,1,0:T(8,128)S(1)}, u32[]{:S(2)}, u32[]{:S(2)}) %all-to-all-start) | async-done | bytes 524320 | tf_op jit(solution)/shard_map/all_to_all | solution.py:30
  345.5 0.7 fusion.24
  346.2 0.0 all-gather.5.cloned.1.call-update
  346.2 5.6 %fusion.25 = f32[16,1,512]{2,1,0:T(1,128)S(1)} fusion(bf16[16,512,512]{2,1,0:T(8,128)(2,1)} %param.15, bf16[16,512,1]{1,0,2:T(8,128)(2,1)S(1)} %fusion.31), kind=kOutput, calls=%fused_computation.69 | convolution fusion | flops 8388608 | bytes 8437760 | tf_op jit(solution)/shard_map/mij,mj->mi/dot_general | solution.py:114
  351.8 0.6 copy.18
  352.5 189.4 %all-gather.5.cloned.1.call-done = bf16[2048,512]{1,0:T(8,128)(2,1)} async-done(((bf16[16,512]{1,0:T(8,128)(2,1)}), bf16[2048,512]{1,0:T(8,128)(2,1)}) %all-gather.5.cloned.1.call-update) | async-done | bytes 2097168 | tf_op jit(solution)/shard_map/all_gather | solution.py:107
  541.8 6.2 %subtract_convert_fusion = bf16[1024,512]{1,0:T(8,128)(2,1)} fusion(f32[1024,512]{1,0:T(8,128)S(1)} %get-tuple-element.10, bf16[2048,1024]{0,1:T(8,128)(2,1)} %bitcast.29, bf16[2048,512]{1,0:T(8,128)(2,1)} %all-gather.5.cloned.1.call-done), kind=kOutput, calls=%fused_computation.16 | convolution fusion | flops 2149056512 | bytes 9437184 | tf_op jit(solution)/shard_map/dot_general | solution.py:105
  (23 shorter events, 0.1 us)
Async XLA Ops:
  7.2 204.4 %all-gather.3.cloned.1.call-start = ((), (), s32[]{:S(2)}) async-start(), calls=%async_computation.2 | async-start | bytes 4755456 | tf_op jit(solution)/shard_map/all_gather | solution.py:14
  10.2 319.6 %reduce-scatter.2.cloned.1.call-start = ((), (), s32[]{:S(2)}) async-start(), calls=%async_computation.3 | async-start | bytes 8912896 | tf_op jit(solution)/shard_map/reduce_scatter | solution.py:94
  239.8 7.3 %slice-start = ((s8[4718592]{0:T(1024)(128)(4,1)}), s8[4194304]{0:T(1024)(128)(4,1)S(1)}, s32[]{:S(2)}) async-start(s8[4718592]{0:T(1024)(128)(4,1)} %bitcast.31), calls=%async_computation.5 | async-start | bytes 8388608
  244.0 3.1 slice-start.1
  245.1 2.0 copy-start
  247.1 4.5 copy-start.1
  247.1 4.5 copy-start.2
  259.9 76.5 %copy-start.3 = (s32[16]{0:T(128)S(1)}, s32[16]{0:T(128)}, u32[]{:S(2)}) copy-start(s32[16]{0:T(128)} %param.13) | copy-start | bytes 196
  259.9 76.5 %copy-start.4 = (s32[16]{0:T(128)S(1)}, s32[16]{0:T(128)}, u32[]{:S(2)}) copy-start(s32[16]{0:T(128)} %param.14) | copy-start | bytes 196
  329.8 15.7 %all-to-all-start = ((f32[8,16,1024]{2,1,0:T(8,128)}), f32[8,16,1024]{2,1,0:T(8,128)S(1)}, u32[]{:S(2)}, u32[]{:S(2)}) async-start(f32[8,16,1024]{2,1,0:T(8,128)} %bitcast.33), calls=%async_computation.1 | async-start | bytes 1048576 | tf_op jit(solution)/shard_map/all_to_all | solution.py:30
  336.4 205.4 %all-gather.5.cloned.1.call-start = ((), (), s32[]{:S(2)}) async-start(), calls=%async_computation.4 | async-start | bytes 2113536 | tf_op jit(solution)/shard_map/all_gather | solution.py:107
Sparse Core Ops, SparseCore 0:
  10.3 201.2 all-gather.2
  260.1 69.6 reduce-scatter.1
  346.3 195.4 all-gather.4
where the time goes:
time: 555 us
  waiting for transfers between devices  470 us (85%)
  local copies, waits for them, and re-layouts  26.7 us (5%)
  matrix products  23.5 us (4%)
  other arithmetic  14.1 us (3%)
  between operations  13.9 us (3%)
  starting transfers between devices  6.72 us (1%)
    all_gather x1, waiting for transfers between devices, in_one_piece(): whole, at, done = (lax.all_gather(both, axis, axis=dim, tiled=True), 0, [])  201 us
    all_gather x1, waiting for transfers between devices, on_device(): lax.all_gather(cross_low, ('gx', 'gz'), axis=0, tiled=True)  189 us
    reduce_scatter x1, waiting for transfers between devices, on_device(): lax.psum_scatter(jnp.dot(table, products, preferred_element_type=jnp.floa...  69.8 us
    gather x2, local copies, waits for them, and re-layouts, on_device(): table = patterns(jnp.take(every_x, modes), jnp.take(every_z, modes))  23.6 us
  transfers between devices with their start and end apart: 4, of which 4 were waited for; matrix products, arithmetic and copies ran while one was open for 1% of the time, Pallas kernels for 0%

commit v1 on v0

--- a/solution.py
+++ b/solution.py
@@ -104,7 +104,12 @@
     index_z = every_z
     restored = lax.dot_general(
         patterns(index_x, index_z),
-        lax.all_gather(cross_low, ("gx", "gz"), axis=0, tiled=True),
+        jnp.concatenate(
+            lax.all_to_all(
+                jnp.stack([cross_low] * lax.axis_size(("gx", "gz"))), ("gx", "gz"), 0, 0
+            ),
+            axis=0,
+        ),
         CONTRACT_FIRST,
         preferred_element_type=jnp.float32,
     )

time: 555 us -> 401 us (0.72)
  waiting for transfers between devices: 470 us -> 304 us
  starting transfers between devices: 6.72 us -> 16.8 us
    all_gather x1 -> x0, waiting for transfers between devices: 189 us -> none  [on_device(): lax.all_gather(cross_low, ('gx', 'gz'), axis=0, tiled=True)]
    all_to_all x0 -> x1, waiting for transfers between devices: none -> 24.2 us  [on_device(): lax.all_to_all(jnp.stack([cross_low] * lax.axis_size(('gx', 'gz'))), ('gx...]
    all_to_all x0 -> x1, starting transfers between devices: none -> 10.3 us  [on_device(): lax.all_to_all(jnp.stack([cross_low] * lax.axis_size(('gx', 'gz'))), ('gx...]
  transfers between devices with their start and end apart: 4 -> 4, of which waited for: 4 -> 4; matrix products, arithmetic and copies ran while one was open for 1% -> 2% of each run, Pallas kernels for 0% -> 0%
where the time goes in v1:
time: 401 us
  waiting for transfers between devices  304 us (76%)
  local copies, waits for them, and re-layouts  28.3 us (7%)
  matrix products  23.6 us (6%)
  starting transfers between devices  16.8 us (4%)
  between operations  14.2 us (4%)
  other arithmetic  13.6 us (3%)
    all_gather x1, waiting for transfers between devices, in_one_piece(): whole, at, done = (lax.all_gather(both, axis, axis=dim, tiled=True), 0, [])  201 us
    reduce_scatter x1, waiting for transfers between devices, on_device(): lax.psum_scatter(jnp.dot(table, products, preferred_element_type=jnp.floa...  70 us
    all_to_all x1, waiting for transfers between devices, on_device(): lax.all_to_all(jnp.stack([cross_low] * lax.axis_size(('gx', 'gz'))), ('gx...  24.2 us
    gather x2, local copies, waits for them, and re-layouts, on_device(): table = patterns(jnp.take(every_x, modes), jnp.take(every_z, modes))  23.6 us
    all_to_all x1, starting transfers between devices, on_device(): lax.all_to_all(jnp.stack([cross_low] * lax.axis_size(('gx', 'gz'))), ('gx...  10.3 us
    all_to_all x1, waiting for transfers between devices, sent_and_summed(): pieces = lax.all_to_all(cut_along(x, dim, count), axis, 0, 0, tiled=True)  9.02 us
  transfers between devices with their start and end apart: 4, of which 4 were waited for; matrix products, arithmetic and copies ran while one was open for 2% of the time, Pallas kernels for 0%

profile of v1, /device:TPU:1, one launch (start us, length us, event | category | flops | bytes accessed | tf_op | source)
XLA Modules:
  0.0 400.9 jit_solution(1818045036313394778)
XLA Ops:
  7.2 0.0 all-gather.2.cloned.1.call-start
  7.2 0.7 convert_bitcast_fusion.1
  7.9 0.1 copy.11
  8.0 0.7 convert_bitcast_fusion
  8.6 0.1 copy.12
  8.7 1.4 concatenate.9
  10.2 0.0 all-gather.2.cloned.1.call-update
  10.2 0.0 reduce-scatter.2.cloned.1.call-start
  10.3 201.2 %all-gather.2.cloned.1.call-done = bf16[2048,1026]{1,0:T(8,128)(2,1)} async-done(((bf16[16,1026]{1,0:T(8,128)(2,1)}), bf16[2048,1026]{1,0:T(8,128)(2,1)}) %all-gather.2.cloned.1.call-update) | async-done | bytes 4202512 | tf_op jit(solution)/shard_map/all_gather | solution.py:14
  211.4 2.6 convert_reduce_fusion.1
  214.0 11.8 %gather_fusion.1 = s32[2048]{0:T(1024)S(1)} fusion(s32[2048]{0:T(1024)S(1)} %get-tuple-element.5, s32[2048]{0:T(1024)S(1)} %broadcast_clamp_fusion), kind=kCustom, calls=%fused_computation.1.clone | custom fusion | bytes 24576 | tf_op jit(solution)/shard_map/jit(_take)/gather | solution.py:93
  225.9 11.8 %gather_fusion = s32[2048]{0:T(1024)S(1)} fusion(s32[2048]{0:T(1024)S(1)} %get-tuple-element.3, s32[2048]{0:T(1024)S(1)} %broadcast_clamp_fusion), kind=kCustom, calls=%fused_computation.clone | custom fusion | bytes 24576 | tf_op jit(solution)/shard_map/jit(_take)/gather | solution.py:93
  237.7 2.1 fusion.8
  239.8 4.2 %sine_select_fusion = (f32[2048,32]{0,1:T(8,128)S(1)}, f32[2048,32]{0,1:T(8,128)S(1)}, f32[2048,32]{0,1:T(8,128)S(1)}, f32[2048,32]{0,1:T(8,128)S(1)}) fusion(s32[2048]{0:T(1024)S(1)} %add_select_fusion.4, s32[32]{0:T(128)S(1)} %iota_add_fusion, pred[2048]{0:T(1024)(128)(4,1)S(1)} %select_compare_fusion, s32[2048]{0:T(1024)S(1)} %get-tuple-element.6, ...), kind=kLoop, calls=%fused_computation.61 | loop fusion | flops 3932160 | bytes 1089792 | tf_op jit(solution)/shard_map/jit(_where)/select_n | solution.py:38
  244.0 1.1 multiply_convert_fusion.1
  245.1 1.1 multiply_convert_fusion
  246.2 0.9 copy-done
  247.0 0.0 copy-start.2
  247.1 4.5 %fusion = f32[1024,1024]{1,0:T(8,128)S(1)} fusion(bf16[2048,1024]{0,1:T(8,128)(2,1)S(1)} %bitcast.29, bf16[2048,1026]{1,0:T(8,128)(2,1)S(1)} %bitcast.33), kind=kOutput, calls=%fused_computation.5 | convolution fusion | flops 4294967296 | bytes 12582912 | tf_op jit(solution)/shard_map/dot_general | solution.py:74
  251.6 1.1 fusion.44
  252.6 7.3 %convolution_multiply_fusion = f32[2048,1024]{1,0:T(8,128)} fusion(bf16[2048,1024]{0,1:T(8,128)(2,1)S(1)} %bitcast.31, bf16[1024,512]{1,0:T(8,128)(2,1)S(1)} %get-tuple-element.9, bf16[1024,512]{1,0:T(8,128)(2,1)S(1)} %get-tuple-element.11), kind=kOutput, calls=%fused_computation.4 | convolution fusion | flops 4301258752 | bytes 14680064 | tf_op jit(solution)/shard_map/dot_general | solution.py:95
  259.9 0.0 reduce-scatter.2.cloned.1.call-update
  260.0 70.0 %reduce-scatter.2.cloned.1.call-done = f32[128,1024]{1,0:T(8,128)} async-done(((f32[2048,1024]{1,0:T(8,128)}), f32[128,1024]{1,0:T(8,128)}) %reduce-scatter.2.cloned.1.call-update) | async-done | bytes 524304 | tf_op jit(solution)/shard_map/reduce_scatter | solution.py:94
  330.0 6.4 %all-to-all-start = ((f32[8,16,1024]{2,1,0:T(8,128)}), f32[8,16,1024]{2,1,0:T(8,128)S(1)}, u32[]{:S(2)}, u32[]{:S(2)}) async-start(f32[8,16,1024]{2,1,0:T(8,128)} %bitcast.34), calls=%async_computation.1 | async-start | bytes 1048576 | tf_op jit(solution)/shard_map/all_to_all | solution.py:30
  336.4 9.0 %all-to-all-done = f32[8,16,1024]{2,1,0:T(8,128)S(1)} async-done(((f32[8,16,1024]{2,1,0:T(8,128)}), f32[8,16,1024]{2,1,0:T(8,128)S(1)}, u32[]{:S(2)}, u32[]{:S(2)}) %all-to-all-start) | async-done | bytes 524320 | tf_op jit(solution)/shard_map/all_to_all | solution.py:30
  345.5 0.1 fusion.24
  345.5 1.6 stack.2
  347.1 10.3 %all-to-all-start.1 = ((bf16[128,16,512]{2,1,0:T(8,128)(2,1)}), bf16[128,16,512]{2,1,0:T(8,128)(2,1)}, u32[]{:S(2)}, u32[]{:S(2)}) async-start(bf16[128,16,512]{2,1,0:T(8,128)(2,1)} %stack.2), calls=%async_computation.2 | async-start | bytes 4194304 | tf_op jit(solution)/shard_map/all_to_all | solution.py:108
  357.4 5.6 %fusion.25 = f32[16,1,512]{2,1,0:T(1,128)S(1)} fusion(bf16[16,512,512]{2,1,0:T(8,128)(2,1)} %param.15, bf16[16,512,1]{1,0,2:T(8,128)(2,1)S(1)} %fusion.31), kind=kOutput, calls=%fused_computation.69 | convolution fusion | flops 8388608 | bytes 8437760 | tf_op jit(solution)/shard_map/mij,mj->mi/dot_general | solution.py:119
  363.0 0.6 copy.18
  363.7 24.2 %all-to-all-done.1 = bf16[128,16,512]{2,1,0:T(8,128)(2,1)} async-done(((bf16[128,16,512]{2,1,0:T(8,128)(2,1)}), bf16[128,16,512]{2,1,0:T(8,128)(2,1)}, u32[]{:S(2)}, u32[]{:S(2)}) %all-to-all-start.1) | async-done | bytes 2097184 | tf_op jit(solution)/shard_map/all_to_all | solution.py:108
  387.9 6.2 %subtract_convert_fusion = bf16[1024,512]{1,0:T(8,128)(2,1)} fusion(f32[1024,512]{1,0:T(8,128)S(1)} %get-tuple-element.10, bf16[2048,1024]{0,1:T(8,128)(2,1)} %bitcast.30, bf16[2048,512]{1,0:T(8,128)(2,1)} %bitcast.9), kind=kOutput, calls=%fused_computation.16 | convolution fusion | flops 2149056512 | bytes 9437184 | tf_op jit(solution)/shard_map/dot_general | solution.py:105
  (23 shorter events, 0.1 us)
Async XLA Ops:
  7.2 204.3 %all-gather.2.cloned.1.call-start = ((), (), s32[]{:S(2)}) async-start(), calls=%async_computation.3 | async-start | bytes 4755456 | tf_op jit(solution)/shard_map/all_gather | solution.py:14
  10.2 319.8 %reduce-scatter.2.cloned.1.call-start = ((), (), s32[]{:S(2)}) async-start(), calls=%async_computation.4 | async-start | bytes 8912896 | tf_op jit(solution)/shard_map/reduce_scatter | solution.py:94
  239.8 7.3 %slice-start = ((s8[4718592]{0:T(1024)(128)(4,1)}), s8[4194304]{0:T(1024)(128)(4,1)S(1)}, s32[]{:S(2)}) async-start(s8[4718592]{0:T(1024)(128)(4,1)} %bitcast.32), calls=%async_computation.5 | async-start | bytes 8388608
  244.0 3.1 slice-start.1
  245.1 2.0 copy-start
  247.0 4.5 %copy-start.1 = (bf16[32,32,512]{2,1,0:T(8,128)(2,1)S(1)}, bf16[32,32,512]{2,1,0:T(8,128)(2,1)}, u32[]{:S(2)}) copy-start(bf16[32,32,512]{2,1,0:T(8,128)(2,1)} %param.9) | copy-start | bytes 3145732
  247.0 4.5 %copy-start.2 = (bf16[32,32,512]{2,1,0:T(8,128)(2,1)S(1)}, bf16[32,32,512]{2,1,0:T(8,128)(2,1)}, u32[]{:S(2)}) copy-start(bf16[32,32,512]{2,1,0:T(8,128)(2,1)} %param.10) | copy-start | bytes 3145732
  259.9 76.5 %copy-start.3 = (s32[16]{0:T(128)S(1)}, s32[16]{0:T(128)}, u32[]{:S(2)}) copy-start(s32[16]{0:T(128)} %param.13) | copy-start | bytes 196
  259.9 76.5 %copy-start.4 = (s32[16]{0:T(128)S(1)}, s32[16]{0:T(128)}, u32[]{:S(2)}) copy-start(s32[16]{0:T(128)} %param.14) | copy-start | bytes 196
  330.0 15.5 %all-to-all-start = ((f32[8,16,1024]{2,1,0:T(8,128)}), f32[8,16,1024]{2,1,0:T(8,128)S(1)}, u32[]{:S(2)}, u32[]{:S(2)}) async-start(f32[8,16,1024]{2,1,0:T(8,128)} %bitcast.34), calls=%async_computation.1 | async-start | bytes 1048576 | tf_op jit(solution)/shard_map/all_to_all | solution.py:30
  347.1 40.8 %all-to-all-start.1 = ((bf16[128,16,512]{2,1,0:T(8,128)(2,1)}), bf16[128,16,512]{2,1,0:T(8,128)(2,1)}, u32[]{:S(2)}, u32[]{:S(2)}) async-start(bf16[128,16,512]{2,1,0:T(8,128)(2,1)} %stack.2), calls=%async_computation.2 | async-start | bytes 4194304 | tf_op jit(solution)/shard_map/all_to_all | solution.py:108
Sparse Core Ops, SparseCore 0:
  10.3 201.0 all-gather.1
  260.1 69.8 reduce-scatter.1
